TPU v7x, 32 devices: a whole 2x2x4 slice. The times are simulated.
32 devices in a mesh: north: 8 (over z, x), deep: 4 (over y, core).
Axes of the slice: x: 2, y: 2, z: 4, core: 2. Of those that a mesh axis runs over, the one named last changes fastest.
Arguments:
- source: float32 [128, 128, 2048], P(None, 'north', 'deep'), may hold values from -6 to 6
- symbol_x: float32 [128], replicated, may hold values from 0.3 to 3
- symbol_y: float32 [128], replicated, may hold values from 0.3 to 3
- symbol_z: float32 [2048], replicated, may hold values from 0.3 to 3
Outputs:
- coefficients: float32 [64, 64, 1024], P('north', 'deep')
All inputs are finite; a program needn't handle non-finite values.
Results may differ from a plain program's by a relative error of at most 0.000071.
Values sent between devices are 32-bit elements; how exact they have to be, the bound alone decides.
A program may use at most 128 MiB of HBM per device.

v0:
```python
import jax
import jax.numpy as jnp
import numpy as np
from jax import lax
from jax.sharding import PartitionSpec as P

HIGH = lax.Precision.HIGH


def small_table(rows, modes, count):
    rank = np.outer(rows, modes) % (2 * count + 2)
    return np.pi / (count + 1) * rank


def kept_table(count):
    angle = small_table(np.arange(1, count + 1), np.arange(1, count // 2 + 1), count)
    return jnp.asarray((np.sin(angle) * (2.0 / (count + 1)) ** 0.5).astype(np.float32))


def long_table(count, fine=32):
    modes = np.arange(1, count // 2 + 1)
    gain = (2.0 / (count + 1)) ** 0.5
    coarse = small_table(np.arange(0, count, fine), modes, count)
    step = small_table(np.arange(1, fine + 1), modes, count)
    f32 = lambda v: jnp.asarray(v.astype(np.float32))
    sin_a, cos_a = (f32(np.sin(coarse) * gain), f32(np.cos(coarse) * gain))
    sin_b, cos_b = (f32(np.sin(step)), f32(np.cos(step)))
    table = sin_a[:, None, :] * cos_b[None] + cos_a[:, None, :] * sin_b[None]
    return table.reshape(count, count // 2)


def on_device(source, symbol_x, symbol_y, symbol_z):
    north, deep = (lax.axis_size("north"), lax.axis_size("deep"))
    nx, ny_part, nz_part = source.shape
    each = nx // 2 // north // deep
    v = jnp.einsum("xk,xyz->kyz", kept_table(nx), source, precision=HIGH)
    v = v.reshape(north, deep, each, ny_part, nz_part)
    v = lax.all_to_all(v, "deep", split_axis=1, concat_axis=4, tiled=True)
    v = v.reshape(north, each, ny_part, nz_part * deep)
    v = jnp.einsum("neyz,zk->neyk", v, long_table(nz_part * deep), precision=HIGH)
    v = lax.all_to_all(v, "north", split_axis=0, concat_axis=2, tiled=True)
    v = v.reshape(each, ny_part * north, v.shape[-1])
    v = jnp.einsum("eyz,yk->ekz", v, kept_table(ny_part * north), precision=HIGH)
    v = lax.all_to_all(v, "deep", split_axis=1, concat_axis=0, tiled=True)
    part_x = lax.dynamic_slice_in_dim(symbol_x, lax.axis_index("north") * v.shape[0], v.shape[0])
    part_y = lax.dynamic_slice_in_dim(symbol_y, lax.axis_index("deep") * v.shape[1], v.shape[1])
    symbol = part_x[:, None, None] + part_y[None, :, None] + symbol_z[: v.shape[2]][None, None, :]
    return v * lax.rsqrt(symbol)


def solution(mesh):
    in_specs = (P(None, "north", "deep"), P(), P(), P())
    out_specs = P("north", "deep", None)
    return jax.shard_map(
        on_device, mesh=mesh, in_specs=in_specs, out_specs=out_specs, check_vma=False
    )
```

profile of v0, /device:TPU:0, one launch (start us, length us, event | category | flops | bytes accessed | tf_op | source)
XLA Modules:
  0.0 101.3 jit_solution(16082460734918682209)
XLA Ops:
  0.0 5.6 %fusion = f32[64,16,512]{2,0,1:T(8,128)S(1)} fusion(f32[128,64,1]{0,1,2:T(8,128)} %constant.32, f32[128,16,512]{2,1,0:T(8,128)} %param.10), kind=kOutput, calls=%fused_computation.1 | convolution fusion | flops 402653184 | bytes 6324224 | tf_op jit(solution)/shard_map/xk,xyz->kyz/dot_general | solution.py:36
  5.7 2.3 %reshape.69 = f32[8,4,2,16,512]{4,2,1,0,3:T(2,128)} reshape(f32[64,16,512]{2,0,1:T(8,128)S(1)} %fusion) | data formatting | bytes 4194304 | tf_op jit(solution)/shard_map/reshape | solution.py:37
  7.9 4.3 %copy.19 = f32[8,4,2,16,512]{4,2,0,3,1:T(2,128)} copy(f32[8,4,2,16,512]{4,2,1,0,3:T(2,128)} %reshape.69) | data formatting | bytes 4194304 | tf_op jit(solution)/shard_map/reshape | solution.py:37
  12.2 4.3 %all-to-all-start = ((f32[8,4,2,16,512]{4,2,0,3,1:T(2,128)}), f32[8,4,2,16,512]{4,2,0,3,1:T(2,128)S(1)}, u32[]{:S(2)}, u32[]{:S(2)}) async-start(f32[8,4,2,16,512]{4,2,0,3,1:T(2,128)} %copy.19), calls=%async_computation | async-start | bytes 4194304 | tf_op jit(solution)/shard_map/all_to_all | solution.py:38
  16.5 4.6 %multiply_add_fusion = f32[64,32,1024]{2,1,0:T(8,128)} fusion(f32[32,1024]{1,0:T(8,128)S(1)} %copy-done.2, f32[64,1024]{1,0:T(8,128)S(1)} %copy-done, f32[32,1024]{1,0:T(8,128)S(1)} %copy-done.3, f32[64,1024]{1,0:T(8,128)S(1)} %copy-done.1), kind=kLoop, calls=%fused_computation | loop fusion | flops 6291456 | bytes 9175040 | tf_op jit(solution)/shard_map/add | solution.py:28
  21.1 21.0 %all-to-all-done = f32[8,4,2,16,512]{4,2,0,3,1:T(2,128)S(1)} async-done(((f32[8,4,2,16,512]{4,2,0,3,1:T(2,128)}), f32[8,4,2,16,512]{4,2,0,3,1:T(2,128)S(1)}, u32[]{:S(2)}, u32[]{:S(2)}) %all-to-all-start) | async-done | bytes 2097184 | tf_op jit(solution)/shard_map/all_to_all | solution.py:38
  42.2 2.7 %copy.20 = f32[8,1,2,16,4,512]{5,4,3,2,0,1:T(4,128)} copy(f32[8,1,2,16,4,512]{5,2,0,3,4,1:T(2,128)S(1)} %bitcast.30) | data formatting | bytes 4194304 | tf_op jit(solution)/shard_map/all_to_all | solution.py:38
  44.9 2.7 %reshape.70 = f32[8,2,16,2048]{3,2,1,0:T(8,128)S(1)} reshape(f32[8,1,2,16,4,512]{5,4,3,2,0,1:T(4,128)} %copy.20) | data formatting | bytes 4194304 | tf_op jit(solution)/shard_map/reshape | solution.py:39
  47.6 6.5 %fusion.2 = f32[8,2,16,1024]{3,2,1,0:T(8,128)S(1)} fusion(f32[8,2,16,2048]{3,2,1,0:T(8,128)S(1)} %reshape.70, f32[2048,1024,1,1]{1,0,3,2:T(8,128)} %bitcast.29), kind=kOutput, calls=%fused_computation.6 | convolution fusion | flops 3221225472 | bytes 11534336 | tf_op jit(solution)/shard_map/neyz,zk->neyk/dot_general | solution.py:40
  54.0 0.0 copy-start.4
  54.1 0.0 copy-start.5
  54.1 0.0 copy-start.6
  54.1 0.0 slice-start
  54.1 32.0 %all_to_all.48 = f32[8,2,16,1024]{3,2,1,0:T(8,128)S(1)} all-to-all(f32[8,2,16,1024]{3,2,1,0:T(8,128)S(1)} %fusion.2), channel_id=1, replica_groups=mesh['north'=8,'deep'=4] {'north'}, dimensions={0} | all-to-all | bytes 2097152 | tf_op jit(solution)/shard_map/all_to_all | solution.py:41
  86.1 0.1 copy.21
  86.2 0.4 convolution_bitcast_fusion
  86.7 1.2 %copy.22 = f32[2,64,1024]{2,0,1:T(2,128)} copy(f32[2,64,1024]{2,1,0:T(8,128)S(1)} %convolution_bitcast_fusion) | data formatting | bytes 1048576 | tf_op jit(solution)/shard_map/eyz,yk->ekz/transpose | solution.py:43
  87.9 3.5 %all-to-all-start.2 = ((f32[2,64,1024]{2,0,1:T(2,128)}), f32[2,64,1024]{2,0,1:T(2,128)S(1)}, u32[]{:S(2)}, u32[]{:S(2)}) async-start(f32[2,64,1024]{2,0,1:T(2,128)} %copy.22), calls=%async_computation.2 | async-start | bytes 1048576 | tf_op jit(solution)/shard_map/all_to_all | solution.py:44
  91.4 0.1 dynamic_slice.7
  91.5 0.1 dynamic_slice.6
  91.5 0.1 broadcast_add_fusion
  91.6 8.5 %all-to-all-done.2 = f32[2,64,1024]{2,0,1:T(2,128)S(1)} async-done(((f32[2,64,1024]{2,0,1:T(2,128)}), f32[2,64,1024]{2,0,1:T(2,128)S(1)}, u32[]{:S(2)}, u32[]{:S(2)}) %all-to-all-start.2) | async-done | bytes 524320 | tf_op jit(solution)/shard_map/all_to_all | solution.py:44
  100.1 0.2 copy.23
  100.3 0.9 bitcast_multiply_fusion
  (12 shorter events, 0.0 us)
Async XLA Ops:
  7.9 8.5 %copy-start = (f32[64,1024]{1,0:T(8,128)S(1)}, f32[64,1024]{1,0:T(8,128)}, u32[]{:S(2)}) copy-start(f32[64,1024]{1,0:T(8,128)} %constant.29.clone) | copy-start | bytes 786436
  7.9 8.5 %copy-start.1 = (f32[64,1024]{1,0:T(8,128)S(1)}, f32[64,1024]{1,0:T(8,128)}, u32[]{:S(2)}) copy-start(f32[64,1024]{1,0:T(8,128)} %constant.28.clone) | copy-start | bytes 786436
  7.9 8.5 %copy-start.2 = (f32[32,1024]{1,0:T(8,128)S(1)}, f32[32,1024]{1,0:T(8,128)}, u32[]{:S(2)}) copy-start(f32[32,1024]{1,0:T(8,128)} %constant.30.clone) | copy-start | bytes 393220
  7.9 8.6 %copy-start.3 = (f32[32,1024]{1,0:T(8,128)S(1)}, f32[32,1024]{1,0:T(8,128)}, u32[]{:S(2)}) copy-start(f32[32,1024]{1,0:T(8,128)} %constant.31.clone) | copy-start | bytes 393220
  12.2 29.9 %all-to-all-start = ((f32[8,4,2,16,512]{4,2,0,3,1:T(2,128)}), f32[8,4,2,16,512]{4,2,0,3,1:T(2,128)S(1)}, u32[]{:S(2)}, u32[]{:S(2)}) async-start(f32[8,4,2,16,512]{4,2,0,3,1:T(2,128)} %copy.19), calls=%async_computation | async-start | bytes 4194304 | tf_op jit(solution)/shard_map/all_to_all | solution.py:38
  54.0 32.2 %copy-start.4 = (f32[128,64,1]{0,1,2:T(8,128)S(1)}, f32[128,64,1]{0,1,2:T(8,128)}, u32[]{:S(2)}) copy-start(f32[128,64,1]{0,1,2:T(8,128)} %constant.32) | copy-start | bytes 98308
  54.1 37.3 %copy-start.5 = (f32[128]{0:T(128)S(1)}, f32[128]{0:T(128)}, u32[]{:S(2)}) copy-start(f32[128]{0:T(128)} %param.12) | copy-start | bytes 1540
  54.1 37.4 %copy-start.6 = (f32[128]{0:T(128)S(1)}, f32[128]{0:T(128)}, u32[]{:S(2)}) copy-start(f32[128]{0:T(128)} %param.11) | copy-start | bytes 1540
  54.1 46.2 %slice-start = ((f32[2048]{0:T(1024)}), f32[1024]{0:T(1024)S(1)}, s32[]{:S(2)}) async-start(f32[2048]{0:T(1024)} %param.13), calls=%async_computation.3 | async-start | bytes 8192 | tf_op jit(solution)/shard_map/slice | solution.py:47
  87.9 12.3 %all-to-all-start.2 = ((f32[2,64,1024]{2,0,1:T(2,128)}), f32[2,64,1024]{2,0,1:T(2,128)S(1)}, u32[]{:S(2)}, u32[]{:S(2)}) async-start(f32[2,64,1024]{2,0,1:T(2,128)} %copy.22), calls=%async_computation.2 | async-start | bytes 1048576 | tf_op jit(solution)/shard_map/all_to_all | solution.py:44
where the time goes:
time: 102 us; the launch traced here: 101 us
  blocking collectives  32 us (31%)
  waiting for transfers between devices  29.6 us (29%)
  local copies, waits for them, and re-layouts  13.6 us (13%)
  matrix products  12.5 us (12%)
  starting transfers between devices  7.74 us (8%)
  other arithmetic  5.65 us (6%)
    all_to_all x1, blocking collectives, on_device(): v = lax.all_to_all(v, 'north', split_axis=0, concat_axis=2, tiled=True)  32 us
    all_to_all x1, waiting for transfers between devices, on_device(): v = lax.all_to_all(v, 'deep', split_axis=1, concat_axis=4, tiled=True)  21 us
    all_to_all x1, waiting for transfers between devices, on_device(): v = lax.all_to_all(v, 'deep', split_axis=1, concat_axis=0, tiled=True)  8.54 us
    reshape x2, local copies, waits for them, and re-layouts, on_device(): v = v.reshape(north, deep, each, ny_part, nz_part)  6.54 us
    dot_general x1, matrix products, on_device(): jnp.einsum('neyz,zk->neyk', v, long_table(nz_part * deep), precision=HIGH)  6.47 us
    dot_general x1, matrix products, on_device(): v = jnp.einsum('xk,xyz->kyz', kept_table(nx), source, precision=HIGH)  5.65 us
    add x1, other arithmetic, long_table(): table = sin_a[:, None, :] * cos_b[None] + cos_a[:, None, :] * sin_b[None]  4.63 us
    all_to_all x1, starting transfers between devices, on_device(): v = lax.all_to_all(v, 'deep', split_axis=1, concat_axis=4, tiled=True)  4.27 us
  transfers between devices with their start and end apart: 2, of which 2 were waited for; matrix products, arithmetic and copies ran while one was open for 5% of the time, Pallas kernels for 0%

commit v1 on v0

--- a/solution.py
+++ b/solution.py
@@ -5,6 +5,14 @@
 from jax.sharding import PartitionSpec as P
 
 HIGH = lax.Precision.HIGH
+
+
+def choose_trees(group_axis, packet):
+    e_next = lax.all_to_all(
+        jnp.stack(jnp.split(packet, lax.axis_size(group_axis), axis=0)), group_axis, 0, 0
+    )
+    a_next = jnp.concatenate(e_next, axis=2)
+    return a_next
 
 
 def small_table(rows, modes, count):
@@ -38,7 +46,7 @@
     v = lax.all_to_all(v, "deep", split_axis=1, concat_axis=4, tiled=True)
     v = v.reshape(north, each, ny_part, nz_part * deep)
     v = jnp.einsum("neyz,zk->neyk", v, long_table(nz_part * deep), precision=HIGH)
-    v = lax.all_to_all(v, "north", split_axis=0, concat_axis=2, tiled=True)
+    v = choose_trees("north", v)
     v = v.reshape(each, ny_part * north, v.shape[-1])
     v = jnp.einsum("eyz,yk->ekz", v, kept_table(ny_part * north), precision=HIGH)
     v = lax.all_to_all(v, "deep", split_axis=1, concat_axis=0, tiled=True)

time: 102 us -> 102 us (level)
  no operation moved by 1% of the time
where the time goes in v1:
time: 102 us; the launch traced here: 101 us
  blocking collectives  31.9 us (31%)
  waiting for transfers between devices  29.6 us (29%)
  local copies, waits for them, and re-layouts  13.7 us (13%)
  matrix products  12.5 us (12%)
  starting transfers between devices  7.74 us (8%)
  other arithmetic  5.65 us (6%)
    all_to_all x1, blocking collectives, choose_trees(): lax.all_to_all(jnp.stack(jnp.split(packet, lax.axis_size(group_axis), axi...  31.9 us
    all_to_all x1, waiting for transfers between devices, on_device(): v = lax.all_to_all(v, 'deep', split_axis=1, concat_axis=4, tiled=True)  21 us
    all_to_all x1, waiting for transfers between devices, on_device(): v = lax.all_to_all(v, 'deep', split_axis=1, concat_axis=0, tiled=True)  8.54 us
    reshape x2, local copies, waits for them, and re-layouts, on_device(): v = v.reshape(north, deep, each, ny_part, nz_part)  6.54 us
    dot_general x1, matrix products, on_device(): jnp.einsum('neyz,zk->neyk', v, long_table(nz_part * deep), precision=HIGH)  6.47 us
    dot_general x1, matrix products, on_device(): v = jnp.einsum('xk,xyz->kyz', kept_table(nx), source, precision=HIGH)  5.65 us
    add x1, other arithmetic, long_table(): table = sin_a[:, None, :] * cos_b[None] + cos_a[:, None, :] * sin_b[None]  4.63 us
    all_to_all x1, starting transfers between devices, on_device(): v = lax.all_to_all(v, 'deep', split_axis=1, concat_axis=4, tiled=True)  4.27 us
  transfers between devices with their start and end apart: 2, of which 2 were waited for; matrix products, arithmetic and copies ran while one was open for 5% of the time, Pallas kernels for 0%

profile of v1, /device:TPU:0, one launch (start us, length us, event | category | flops | bytes accessed | tf_op | source)
XLA Modules:
  0.0 101.3 jit_solution(593309127478340535)
XLA Ops:
  0.0 5.6 %fusion = f32[64,16,512]{2,0,1:T(8,128)S(1)} fusion(f32[128,64,1]{0,1,2:T(8,128)} %constant.32, f32[128,16,512]{2,1,0:T(8,128)} %param.10), kind=kOutput, calls=%fused_computation.1 | convolution fusion | flops 402653184 | bytes 6324224 | tf_op jit(solution)/shard_map/xk,xyz->kyz/dot_general | solution.py:44
  5.7 2.3 %reshape.68 = f32[8,4,2,16,512]{4,2,1,0,3:T(2,128)} reshape(f32[64,16,512]{2,0,1:T(8,128)S(1)} %fusion) | data formatting | bytes 4194304 | tf_op jit(solution)/shard_map/reshape | solution.py:45
  7.9 4.3 %copy.19 = f32[8,4,2,16,512]{4,2,0,3,1:T(2,128)} copy(f32[8,4,2,16,512]{4,2,1,0,3:T(2,128)} %reshape.68) | data formatting | bytes 4194304 | tf_op jit(solution)/shard_map/reshape | solution.py:45
  12.2 4.3 %all-to-all-start = ((f32[8,4,2,16,512]{4,2,0,3,1:T(2,128)}), f32[8,4,2,16,512]{4,2,0,3,1:T(2,128)S(1)}, u32[]{:S(2)}, u32[]{:S(2)}) async-start(f32[8,4,2,16,512]{4,2,0,3,1:T(2,128)} %copy.19), calls=%async_computation | async-start | bytes 4194304 | tf_op jit(solution)/shard_map/all_to_all | solution.py:46
  16.5 4.6 %multiply_add_fusion = f32[64,32,1024]{2,1,0:T(8,128)} fusion(f32[32,1024]{1,0:T(8,128)S(1)} %copy-done.2, f32[64,1024]{1,0:T(8,128)S(1)} %copy-done.1, f32[32,1024]{1,0:T(8,128)S(1)} %copy-done.3, f32[64,1024]{1,0:T(8,128)S(1)} %copy-done), kind=kLoop, calls=%fused_computation | loop fusion | flops 6291456 | bytes 9175040 | tf_op jit(solution)/shard_map/add | solution.py:36
  21.1 21.0 %all-to-all-done = f32[8,4,2,16,512]{4,2,0,3,1:T(2,128)S(1)} async-done(((f32[8,4,2,16,512]{4,2,0,3,1:T(2,128)}), f32[8,4,2,16,512]{4,2,0,3,1:T(2,128)S(1)}, u32[]{:S(2)}, u32[]{:S(2)}) %all-to-all-start) | async-done | bytes 2097184 | tf_op jit(solution)/shard_map/all_to_all | solution.py:46
  42.2 2.7 %copy.20 = f32[8,1,2,16,4,512]{5,4,3,2,0,1:T(4,128)} copy(f32[8,1,2,16,4,512]{5,2,0,3,4,1:T(2,128)S(1)} %bitcast.60) | data formatting | bytes 4194304 | tf_op jit(solution)/shard_map/all_to_all | solution.py:46
  44.9 2.7 %reshape.69 = f32[8,2,16,2048]{3,2,1,0:T(8,128)S(1)} reshape(f32[8,1,2,16,4,512]{5,4,3,2,0,1:T(4,128)} %copy.20) | data formatting | bytes 4194304 | tf_op jit(solution)/shard_map/reshape | solution.py:47
  47.6 6.5 %fusion.10 = f32[8,2,16,1024]{3,2,1,0:T(8,128)S(1)} fusion(f32[8,2,16,2048]{3,2,1,0:T(8,128)S(1)} %reshape.69, f32[2048,1024,1,1]{1,0,3,2:T(8,128)} %bitcast.59), kind=kOutput, calls=%fused_computation.22 | convolution fusion | flops 3221225472 | bytes 11534336 | tf_op jit(solution)/shard_map/neyz,zk->neyk/dot_general | solution.py:48
  54.0 0.0 copy-start.4
  54.2 0.0 copy-start.5
  54.2 0.0 copy-start.6
  54.2 0.0 slice-start
  54.3 31.9 %all_to_all.38 = f32[8,1,2,16,1024]{4,3,2,1,0:T(8,128)S(1)} all-to-all(f32[8,1,2,16,1024]{4,3,2,1,0:T(8,128)S(1)} %fusion.2), channel_id=1, replica_groups=mesh['north'=8,'deep'=4] {'north'}, dimensions={0} | all-to-all | bytes 2097152 | tf_op jit(solution)/shard_map/all_to_all | solution.py:11
  86.2 0.1 copy.21
  86.3 0.4 convolution_bitcast_fusion
  86.7 1.2 %copy.22 = f32[2,64,1024]{2,0,1:T(2,128)} copy(f32[2,64,1024]{2,1,0:T(8,128)S(1)} %convolution_bitcast_fusion) | data formatting | bytes 1048576 | tf_op jit(solution)/shard_map/eyz,yk->ekz/transpose | solution.py:51
  87.9 3.5 %all-to-all-start.2 = ((f32[2,64,1024]{2,0,1:T(2,128)}), f32[2,64,1024]{2,0,1:T(2,128)S(1)}, u32[]{:S(2)}, u32[]{:S(2)}) async-start(f32[2,64,1024]{2,0,1:T(2,128)} %copy.22), calls=%async_computation.2 | async-start | bytes 1048576 | tf_op jit(solution)/shard_map/all_to_all | solution.py:52
  91.4 0.1 dynamic_slice.6
  91.5 0.1 dynamic_slice.7
  91.5 0.1 broadcast_add_fusion
  91.6 8.5 %all-to-all-done.2 = f32[2,64,1024]{2,0,1:T(2,128)S(1)} async-done(((f32[2,64,1024]{2,0,1:T(2,128)}), f32[2,64,1024]{2,0,1:T(2,128)S(1)}, u32[]{:S(2)}, u32[]{:S(2)}) %all-to-all-start.2) | async-done | bytes 524320 | tf_op jit(solution)/shard_map/all_to_all | solution.py:52
  100.2 0.2 copy.23
  100.3 0.9 bitcast_multiply_fusion
  (20 shorter events, 0.1 us)
Async XLA Ops:
  7.9 8.5 %copy-start = (f32[64,1024]{1,0:T(8,128)S(1)}, f32[64,1024]{1,0:T(8,128)}, u32[]{:S(2)}) copy-start(f32[64,1024]{1,0:T(8,128)} %constant.28.clone) | copy-start | bytes 786436
  7.9 8.5 %copy-start.1 = (f32[64,1024]{1,0:T(8,128)S(1)}, f32[64,1024]{1,0:T(8,128)}, u32[]{:S(2)}) copy-start(f32[64,1024]{1,0:T(8,128)} %constant.29.clone) | copy-start | bytes 786436
  7.9 8.5 %copy-start.2 = (f32[32,1024]{1,0:T(8,128)S(1)}, f32[32,1024]{1,0:T(8,128)}, u32[]{:S(2)}) copy-start(f32[32,1024]{1,0:T(8,128)} %constant.30.clone) | copy-start | bytes 393220
  7.9 8.6 %copy-start.3 = (f32[32,1024]{1,0:T(8,128)S(1)}, f32[32,1024]{1,0:T(8,128)}, u32[]{:S(2)}) copy-start(f32[32,1024]{1,0:T(8,128)} %constant.31.clone) | copy-start | bytes 393220
  12.2 29.9 %all-to-all-start = ((f32[8,4,2,16,512]{4,2,0,3,1:T(2,128)}), f32[8,4,2,16,512]{4,2,0,3,1:T(2,128)S(1)}, u32[]{:S(2)}, u32[]{:S(2)}) async-start(f32[8,4,2,16,512]{4,2,0,3,1:T(2,128)} %copy.19), calls=%async_computation | async-start | bytes 4194304 | tf_op jit(solution)/shard_map/all_to_all | solution.py:46
  54.0 32.2 %copy-start.4 = (f32[128,64,1]{0,1,2:T(8,128)S(1)}, f32[128,64,1]{0,1,2:T(8,128)}, u32[]{:S(2)}) copy-start(f32[128,64,1]{0,1,2:T(8,128)} %constant.32) | copy-start | bytes 98308
  54.2 37.2 %copy-start.5 = (f32[128]{0:T(128)S(1)}, f32[128]{0:T(128)}, u32[]{:S(2)}) copy-start(f32[128]{0:T(128)} %param.11) | copy-start | bytes 1540
  54.2 37.3 %copy-start.6 = (f32[128]{0:T(128)S(1)}, f32[128]{0:T(128)}, u32[]{:S(2)}) copy-start(f32[128]{0:T(128)} %param.12) | copy-start | bytes 1540
  54.2 46.1 %slice-start = ((f32[2048]{0:T(1024)}), f32[1024]{0:T(1024)S(1)}, s32[]{:S(2)}) async-start(f32[2048]{0:T(1024)} %param.13), calls=%async_computation.3 | async-start | bytes 8192 | tf_op jit(solution)/shard_map/slice | solution.py:55
  87.9 12.3 %all-to-all-start.2 = ((f32[2,64,1024]{2,0,1:T(2,128)}), f32[2,64,1024]{2,0,1:T(2,128)S(1)}, u32[]{:S(2)}, u32[]{:S(2)}) async-start(f32[2,64,1024]{2,0,1:T(2,128)} %copy.22), calls=%async_computation.2 | async-start | bytes 1048576 | tf_op jit(solution)/shard_map/all_to_all | solution.py:52
